TPU v7x, 256 devices: a whole 4x4x8 slice. The times are simulated.
256 devices in a mesh: gx: 8 (over y, x_lo), gy: 16 (over z, core), gz: 2 (over x_hi).
Axes of the slice: x: 4 (x_hi: 2, x_lo: 2; x = x_hi * 2 + x_lo), y: 4, z: 8, core: 2. Of those that a mesh axis runs over, the one named last changes fastest.
Arguments:
- starting_kelvin: float32 [16, 128, 4096], P(None, 'gx', ('gy', 'gz')), may hold values from -6 to 6
- substance_label: int32 [16, 128, 4096], P(None, 'gx', ('gy', 'gz')), may hold values from 0 to 3
- voxel_source_patch: int32 [16, 128, 4096], P(None, 'gx', ('gy', 'gz')), may hold values from 0 to 15
- substance_traits: float32 [4, 4], replicated, may hold values from 0.5 to 2
- patch_source_intensity: float32 [16], replicated, may hold values from 0 to 8
Outputs:
- warmed_result: float32 [16, 128, 4096], P(None, 'gx', ('gy', 'gz'))
- solution: float32 [3, 16, 128, 4096], P(None, 'gz', 'gx', 'gy')
- residual: float32 [3, 16, 128, 4096], P(None, 'gz', 'gx', 'gy')
All inputs are finite; a program needn't handle non-finite values.
Results may differ from a plain program's by a relative error of at most 0.0029.
Values sent between devices are 32-bit elements; how exact they have to be, the bound alone decides.
A program may use at most 64 MiB of HBM per device.

v0:
```python
import jax
import jax.numpy as jnp
from jax import lax
from jax.sharding import Mesh
from jax.sharding import PartitionSpec as P

HEAT_STEPS = 2
ITERS = 3
GX_GY_GZ = ("gx_0", "gx_1", "gy_0", "gy_1", "gz")
GX = ("gx_0", "gx_1")
GY_GZ = ("gy_0", "gy_1", "gz")
GY = ("gy_0", "gy_1")
time_step = 0.03
anchor_scale = 0.5
strain_gain = 2.0


def over_axes(value, axes):
    for axis in axes:
        value = lax.psum(value, axis)
    return value


def padded(value, sides, width):
    for axis, dim in sides:
        devices, length = (lax.axis_size(axis), value.shape[dim])
        up = [(i, (i + 1) % devices) for i in range(devices - 1)]
        down = [(j, i) for i, j in up]
        last = lax.slice_in_dim(value, length - width, length, axis=dim)
        initial = lax.slice_in_dim(value, 0, width, axis=dim)
        before = lax.ppermute(last, axis, up)
        after = lax.ppermute(initial, axis, down)
        value = jnp.concatenate([before, value, after], axis=dim)
    return value


def lookup(identity, table, count):
    summed = jnp.zeros(identity.shape, jnp.float32)
    for number in range(count):
        summed = summed + jnp.where(identity == number, table[number], jnp.float32(0.0))
    return summed


def conduct(own, other):
    return 2.0 * own * other / jnp.maximum(own + other, 0.25)


def heat_step(padded_temp, padded_cond, power, inverse_cap):
    centre = padded_temp[:, 1:-1, 1:-1]
    own = padded_cond[:, 1:-1, 1:-1]
    layers, rows, columns = centre.shape
    heat_flux = jnp.zeros_like(centre)
    for row_offset, column_offset in ((0, 1), (2, 1), (1, 0), (1, 2)):
        neighbour = padded_temp[
            :, row_offset : row_offset + rows, column_offset : column_offset + columns
        ]
        other = padded_cond[
            :, row_offset : row_offset + rows, column_offset : column_offset + columns
        ]
        heat_flux = heat_flux + conduct(own, other) * (neighbour - centre)
    vertical_temp = jnp.pad(centre, ((1, 1), (0, 0), (0, 0)))
    vertical_cond = jnp.pad(own, ((1, 1), (0, 0), (0, 0)))
    for layer_offset in (0, 2):
        other = vertical_cond[layer_offset : layer_offset + layers]
        neighbour = vertical_temp[layer_offset : layer_offset + layers]
        heat_flux = heat_flux + conduct(own, other) * (neighbour - centre)
    return centre + time_step * inverse_cap * (heat_flux + power)


def crop(array, margin):
    return array[:, margin : array.shape[1] - margin, margin : array.shape[2] - margin]


def neighbour_offsets():
    listed = []
    for along_z in (-1, 0, 1):
        for along_x in (-1, 0, 1):
            for along_y in (-1, 0, 1):
                if along_z != 0 or along_x != 0 or along_y != 0:
                    listed.append((along_z, along_x, along_y))
    return listed


def apply_operator(field, padded_field, modulus, padded_modulus):
    layers, rows, columns = modulus.shape
    parts = [
        anchor_scale * modulus * field[0],
        anchor_scale * modulus * field[1],
        anchor_scale * modulus * field[2],
    ]
    for along_z, along_x, along_y in neighbour_offsets():
        length_sq = along_z * along_z + along_x * along_x + along_y * along_y
        window = (
            slice(1 + along_z, 1 + along_z + layers),
            slice(1 + along_x, 1 + along_x + rows),
            slice(1 + along_y, 1 + along_y + columns),
        )
        weight = 0.5 / length_sq * (modulus + padded_modulus[window])
        change = [field[index_c] - padded_field[index_c][window] for index_c in range(3)]
        projected = (along_z * change[0] + along_x * change[1] + along_y * change[2]) / length_sq
        for index_c, direction_part in enumerate((along_z, along_x, along_y)):
            parts[index_c] = parts[index_c] + weight * (
                0.5 * change[index_c] + direction_part * projected
            )
    return jnp.stack(parts)


def thermal_load(modulus, padded_modulus, strain, padded_strain):
    layers, rows, columns = modulus.shape
    parts = [jnp.zeros_like(modulus), jnp.zeros_like(modulus), jnp.zeros_like(modulus)]
    for along_z, along_x, along_y in neighbour_offsets():
        length_sq = along_z * along_z + along_x * along_x + along_y * along_y
        window = (
            slice(1 + along_z, 1 + along_z + layers),
            slice(1 + along_x, 1 + along_x + rows),
            slice(1 + along_y, 1 + along_y + columns),
        )
        weight = 0.5 / length_sq * (modulus + padded_modulus[window])
        pushing = weight * (0.5 * (strain + padded_strain[window]))
        for index_c, direction_part in enumerate((along_z, along_x, along_y)):
            if direction_part != 0:
                parts[index_c] = parts[index_c] - strain_gain * direction_part * pushing
    return jnp.stack(parts)


def two_products(residual, image):
    return (
        over_axes(jnp.sum(residual * residual), GX_GY_GZ),
        over_axes(jnp.sum(residual * image), GX_GY_GZ),
    )


def per_device(
    starting_kelvin, substance_label, voxel_source_patch, substance_traits, patch_source_intensity
):
    count = substance_traits.shape[1]
    diffusive_coefficient = lookup(substance_label, substance_traits[0], count)
    inverse_cap = 1.0 / lookup(substance_label, substance_traits[1], count)
    power = lookup(voxel_source_patch, patch_source_intensity, patch_source_intensity.shape[0])
    padded_array = padded(
        jnp.stack([starting_kelvin, diffusive_coefficient, power, inverse_cap]),
        ((GX, 2), (GY_GZ, 3)),
        HEAT_STEPS,
    )
    warmed_result = padded_array[0]
    for number in range(HEAT_STEPS):
        warmed_result = heat_step(
            warmed_result,
            crop(padded_array[1], number),
            crop(padded_array[2], number + 1),
            crop(padded_array[3], number + 1),
        )
    modulus = lookup(substance_label, substance_traits[2], count)
    strain = lookup(substance_label, substance_traits[3], count) * warmed_result
    fields = jnp.stack([modulus, strain])
    fields = lax.all_to_all(fields, "gz", split_axis=1, concat_axis=3, tiled=True)
    padded_fields = padded(fields, ((GX, 2), (GY, 3), ("gz", 1)), 1)

    def extend(field):
        return padded(field, ((GX, 2), (GY, 3), ("gz", 1)), 1)

    modulus = fields[0]
    padded_modulus = padded_fields[0]
    load = thermal_load(modulus, padded_modulus, fields[1], padded_fields[1])

    def operate(field):
        return apply_operator(field, extend(field), modulus, padded_modulus)

    solution = jnp.zeros_like(load)
    residual = load
    image = operate(residual)
    norm_now, product = two_products(residual, image)
    alpha = norm_now / product
    direction, along_image = (residual, image)
    for number in range(ITERS):
        solution = solution + alpha * direction
        residual = residual - alpha * along_image
        if number + 1 < ITERS:
            image = operate(residual)
            norm_next, product = two_products(residual, image)
            ratio = norm_next / norm_now
            alpha = norm_next / (product - ratio * norm_next / alpha)
            direction = residual + ratio * direction
            along_image = image + ratio * along_image
            norm_now = norm_next
    return (warmed_result, solution, residual)


def solution(mesh):
    split = Mesh(
        mesh.devices.reshape(4, 2, 8, 2, mesh.shape["gz"]), ("gx_0", "gx_1", "gy_0", "gy_1", "gz")
    )
    placed = (P(None, GX, GY_GZ), P(None, GX, GY_GZ), P(None, GX, GY_GZ), P(), P())
    return jax.shard_map(
        per_device,
        mesh=split,
        in_specs=placed,
        out_specs=(P(None, GX, GY_GZ), P(None, "gz", GX, GY), P(None, "gz", GX, GY)),
        check_vma=False,
    )
```

profile of v0, /device:TPU:1, one launch (start us, length us, event | category | flops | bytes accessed | tf_op | source)
XLA Modules:
  0.0 349.6 jit_solution(3957960679545552829)
XLA Ops:
  8.0 5.2 %add_bitcast_fusion.11 = (f32[1,16,16,128]{3,1,2,0:T(8,128)S(1)}, f32[1,16,16,128]{3,1,2,0:T(8,128)S(1)}) fusion(pred[16,16,128]{2,0,1:T(8,128)(4,1)S(1)} %get-tuple-element.98, pred[16,16,128]{2,0,1:T(8,128)(4,1)S(1)} %get-tuple-element.97, pred[16,16,128]{2,0,1:T(8,128)(4,1)S(1)} %get-tuple-element.96, pred[16,16,128]{2,0,1:T(8,128)(4,1)S(1)} %get-tuple-element.95, ...), kind=kLoop, calls=%fused_computation.621 | loop fusion | flops 491520 | bytes 393248 | tf_op jit(solution)/shard_map/stack | solution.py:141
  13.2 11.3 %copy_bitcast_fusion = (f32[1,16,16,128]{3,1,2,0:T(8,128)S(1)}, f32[1,16,16,128]{3,1,2,0:T(8,128)S(1)}) fusion(f32[16,16,128]{2,1,0:T(8,128)} %param.5, f32[]{:T(128)} %bitcast.21, f32[]{:T(128)} %bitcast.20, f32[]{:T(128)} %bitcast.19, f32[]{:T(128)} %bitcast.18, f32[]{:T(128)} %bitcast.17, f32[]{:T(128)} %bitcast.16, f32[]{:T(128)} %bitcast.15, ...), kind=kLoop, calls=%fused_computation.521 | loop fusion | flops 1540096 | bytes 524352 | tf_op jit(solution)/shard_map/stack | solution.py:141
  34.2 4.5 %collective-permute-start.2 = (f32[4,16,20,2]{2,1,3,0:T(8,128)S(1)}, f32[4,16,20,2]{2,1,3,0:T(8,128)S(1)}, u32[]{:S(2)}, u32[]{:S(2)}) collective-permute-start(f32[4,16,20,2]{2,1,3,0:T(8,128)S(1)} %copy.202), channel_id=1, source_target_pairs={{0,1},{1,2},{2,3},{3,4},{4,5},{5,6},{6,7},{7,8},{8,9},{9,10},{10,1... | collective-permute-start | bytes 30728 | tf_op jit(solution)/shard_map/ppermute | solution.py:31
  52.1 12.7 %all_to_all.18 = f32[2,16,16,128]{3,2,0,1:T(8,128)S(1)} all-to-all(f32[2,16,16,128]{3,2,0,1:T(8,128)S(1)} %copy.206), channel_id=1, replica_groups=mesh['gx_0'=4,'gx_1'=2,'gy_0'=8,'gy_1'=2,'gz'=2] {'gz'}, dimensions={1} | all-to-all | bytes 524288 | tf_op jit(solution)/shard_map/all_to_all | solution.py:156
  73.4 5.2 %collective-permute-start.6 = (f32[2,8,18,1]{3,2,1,0:T(8,128)S(1)}, f32[2,8,18,1]{3,2,1,0:T(8,128)S(1)}, u32[]{:S(2)}, u32[]{:S(2)}) collective-permute-start(f32[2,8,18,1]{3,2,1,0:T(8,128)S(1)} %get-tuple-element.142), channel_id=1, source_target_pairs={{0,2},{2,4},{4,6},{6,8},{8,10},{10,12},{12,14},{14,16},{16,18},{18... | collective-permute-start | bytes 3464 | tf_op jit(solution)/shard_map/ppermute | solution.py:31
  81.2 4.4 %collective-permute-done.7 = f32[2,8,18,1]{3,2,1,0:T(8,128)S(1)} collective-permute-done((f32[2,8,18,1]{3,2,1,0:T(8,128)S(1)}, f32[2,8,18,1]{3,2,1,0:T(8,128)S(1)}, u32[]{:S(2)}, u32[]{:S(2)}) %collective-permute-start.7) | collective-permute-done | bytes 1184 | tf_op jit(solution)/shard_map/ppermute | solution.py:32
  89.5 4.8 %collective-permute-done.9 = f32[2,1,18,258]{3,2,1,0:T(8,128)S(1)} collective-permute-done((f32[2,1,18,258]{3,2,1,0:T(8,128)S(1)}, f32[2,1,18,258]{3,2,1,0:T(8,128)S(1)}, u32[]{:S(2)}, u32[]{:S(2)}) %collective-permute-start.9) | collective-permute-done | bytes 37184 | tf_op jit(solution)/shard_map/ppermute | solution.py:32
  105.3 4.4 %collective-permute-start.12 = (f32[3,8,18,1]{3,2,1,0:T(8,128)S(1)}, f32[3,8,18,1]{3,2,1,0:T(8,128)S(1)}, u32[]{:S(2)}, u32[]{:S(2)}) collective-permute-start(f32[3,8,18,1]{3,2,1,0:T(8,128)S(1)} %get-tuple-element.130), channel_id=1, source_target_pairs={{0,2},{2,4},{4,6},{6,8},{8,10},{10,12},{12,14},{14,16},{16,18},{18... | collective-permute-start | bytes 5192 | tf_op jit(solution)/shard_map/ppermute | solution.py:31
  113.3 4.4 %collective-permute-done.13 = f32[3,8,18,1]{3,2,1,0:T(8,128)S(1)} collective-permute-done((f32[3,8,18,1]{3,2,1,0:T(8,128)S(1)}, f32[3,8,18,1]{3,2,1,0:T(8,128)S(1)}, u32[]{:S(2)}, u32[]{:S(2)}) %collective-permute-start.13) | collective-permute-done | bytes 1760 | tf_op jit(solution)/shard_map/ppermute | solution.py:32
  121.6 5.3 %collective-permute-done.15 = f32[3,1,18,258]{3,2,1,0:T(8,128)S(1)} collective-permute-done((f32[3,1,18,258]{3,2,1,0:T(8,128)S(1)}, f32[3,1,18,258]{3,2,1,0:T(8,128)S(1)}, u32[]{:S(2)}, u32[]{:S(2)}) %collective-permute-start.15) | collective-permute-done | bytes 55760 | tf_op jit(solution)/shard_map/ppermute | solution.py:32
  136.0 7.9 %all-reduce.9 = (f32[]{:T(128)}, f32[]{:T(128)}) all-reduce(f32[]{:T(128)} %get-tuple-element.17, f32[]{:T(128)} %get-tuple-element.16), channel_id=1, replica_groups=mesh['gx_0'=4,'gx_1'=2,'gy_0'=8,'gy_1'=2,'gz'=2] {'gx_0'}, use_global_device_ids=true, to_apply=%region_1.2 | all-reduce | flops 2 | bytes 16 | tf_op jit(solution)/shard_map/psum | solution.py:20
  143.9 4.4 %all-reduce.18 = (f32[]{:T(128)}, f32[]{:T(128)}) all-reduce(f32[]{:T(128)} %get-tuple-element.28, f32[]{:T(128)} %get-tuple-element.29), channel_id=1, replica_groups=mesh['gx_0'=4,'gx_1'=2,'gy_0'=8,'gy_1'=2,'gz'=2] {'gx_1'}, use_global_device_ids=true, to_apply=%region_2.3 | all-reduce | flops 2 | bytes 16 | tf_op jit(solution)/shard_map/psum | solution.py:20
  148.2 17.7 %all-reduce.6 = (f32[]{:T(128)}, f32[]{:T(128)}) all-reduce(f32[]{:T(128)} %get-tuple-element.46, f32[]{:T(128)} %get-tuple-element.47), channel_id=1, replica_groups=mesh['gx_0'=4,'gx_1'=2,'gy_0'=8,'gy_1'=2,'gz'=2] {'gy_0'}, use_global_device_ids=true, to_apply=%region_3.4 | all-reduce | flops 2 | bytes 16 | tf_op jit(solution)/shard_map/psum | solution.py:20
  166.0 8.6 %all-reduce.15 = (f32[]{:T(128)}, f32[]{:T(128)}) all-reduce(f32[]{:T(128)} %get-tuple-element.22, f32[]{:T(128)} %get-tuple-element.23), channel_id=1, replica_groups=mesh['gx_0'=4,'gx_1'=2,'gy_0'=8,'gy_1'=2,'gz'=2] {'gy_1'}, use_global_device_ids=true, to_apply=%region_4.5 | all-reduce | flops 2 | bytes 16 | tf_op jit(solution)/shard_map/psum | solution.py:20
  174.5 5.9 %all-reduce.12 = (f32[]{:T(128)}, f32[]{:T(128)}) all-reduce(f32[]{:T(128)} %get-tuple-element.40, f32[]{:T(128)} %get-tuple-element.41), channel_id=1, replica_groups=mesh['gx_0'=4,'gx_1'=2,'gy_0'=8,'gy_1'=2,'gz'=2] {'gz'}, use_global_device_ids=true, to_apply=%region_5.6 | all-reduce | flops 2 | bytes 16 | tf_op jit(solution)/shard_map/psum | solution.py:20
  190.4 5.2 %collective-permute-start.18 = (f32[3,8,18,1]{3,2,1,0:T(8,128)S(1)}, f32[3,8,18,1]{3,2,1,0:T(8,128)S(1)}, u32[]{:S(2)}, u32[]{:S(2)}) collective-permute-start(f32[3,8,18,1]{3,2,1,0:T(8,128)S(1)} %get-tuple-element.128), channel_id=1, source_target_pairs={{0,2},{2,4},{4,6},{6,8},{8,10},{10,12},{12,14},{14,16},{16,18},{18... | collective-permute-start | bytes 5192 | tf_op jit(solution)/shard_map/ppermute | solution.py:31
  199.2 4.4 %collective-permute-done.19 = f32[3,8,18,1]{3,2,1,0:T(8,128)S(1)} collective-permute-done((f32[3,8,18,1]{3,2,1,0:T(8,128)S(1)}, f32[3,8,18,1]{3,2,1,0:T(8,128)S(1)}, u32[]{:S(2)}, u32[]{:S(2)}) %collective-permute-start.19) | collective-permute-done | bytes 1760 | tf_op jit(solution)/shard_map/ppermute | solution.py:32
  207.7 5.3 %collective-permute-done.21 = f32[3,1,18,258]{3,2,1,0:T(8,128)S(1)} collective-permute-done((f32[3,1,18,258]{3,2,1,0:T(8,128)S(1)}, f32[3,1,18,258]{3,2,1,0:T(8,128)S(1)}, u32[]{:S(2)}, u32[]{:S(2)}) %collective-permute-start.21) | collective-permute-done | bytes 55760 | tf_op jit(solution)/shard_map/ppermute | solution.py:32
  220.2 7.1 %all-reduce.8 = (f32[]{:T(128)}, f32[]{:T(128)}) all-reduce(f32[]{:T(128)} %get-tuple-element.15, f32[]{:T(128)} %get-tuple-element.14), channel_id=1, replica_groups=mesh['gx_0'=4,'gx_1'=2,'gy_0'=8,'gy_1'=2,'gz'=2] {'gx_0'}, use_global_device_ids=true, to_apply=%region_13.14 | all-reduce | flops 2 | bytes 16 | tf_op jit(solution)/shard_map/psum | solution.py:20
  227.3 4.4 %all-reduce.17 = (f32[]{:T(128)}, f32[]{:T(128)}) all-reduce(f32[]{:T(128)} %get-tuple-element.26, f32[]{:T(128)} %get-tuple-element.27), channel_id=1, replica_groups=mesh['gx_0'=4,'gx_1'=2,'gy_0'=8,'gy_1'=2,'gz'=2] {'gx_1'}, use_global_device_ids=true, to_apply=%region_14.15 | all-reduce | flops 2 | bytes 16 | tf_op jit(solution)/shard_map/psum | solution.py:20
  231.7 14.0 %all-reduce.5 = (f32[]{:T(128)}, f32[]{:T(128)}) all-reduce(f32[]{:T(128)} %get-tuple-element.44, f32[]{:T(128)} %get-tuple-element.45), channel_id=1, replica_groups=mesh['gx_0'=4,'gx_1'=2,'gy_0'=8,'gy_1'=2,'gz'=2] {'gy_0'}, use_global_device_ids=true, to_apply=%region_15.16 | all-reduce | flops 2 | bytes 16 | tf_op jit(solution)/shard_map/psum | solution.py:20
  245.7 9.5 %all-reduce.14 = (f32[]{:T(128)}, f32[]{:T(128)}) all-reduce(f32[]{:T(128)} %get-tuple-element.20, f32[]{:T(128)} %get-tuple-element.21), channel_id=1, replica_groups=mesh['gx_0'=4,'gx_1'=2,'gy_0'=8,'gy_1'=2,'gz'=2] {'gy_1'}, use_global_device_ids=true, to_apply=%region_16.17 | all-reduce | flops 2 | bytes 16 | tf_op jit(solution)/shard_map/psum | solution.py:20
  255.2 6.1 %all-reduce.11 = (f32[]{:T(128)}, f32[]{:T(128)}) all-reduce(f32[]{:T(128)} %get-tuple-element.38, f32[]{:T(128)} %get-tuple-element.39), channel_id=1, replica_groups=mesh['gx_0'=4,'gx_1'=2,'gy_0'=8,'gy_1'=2,'gz'=2] {'gz'}, use_global_device_ids=true, to_apply=%region_17.18 | all-reduce | flops 2 | bytes 16 | tf_op jit(solution)/shard_map/psum | solution.py:20
  269.4 4.2 %collective-permute-done.23 = f32[3,8,1,256]{3,2,1,0:T(1,128)S(1)} collective-permute-done((f32[3,8,1,256]{3,2,1,0:T(1,128)S(1)}, f32[3,8,1,256]{3,2,1,0:T(1,128)S(1)}, u32[]{:S(2)}, u32[]{:S(2)}) %collective-permute-start.23) | collective-permute-done | bytes 24608 | tf_op jit(solution)/shard_map/ppermute | solution.py:32
  273.8 5.0 %collective-permute-start.24 = (f32[3,8,18,1]{3,2,1,0:T(8,128)S(1)}, f32[3,8,18,1]{3,2,1,0:T(8,128)S(1)}, u32[]{:S(2)}, u32[]{:S(2)}) collective-permute-start(f32[3,8,18,1]{3,2,1,0:T(8,128)S(1)} %get-tuple-element.126), channel_id=1, source_target_pairs={{0,2},{2,4},{4,6},{6,8},{8,10},{10,12},{12,14},{14,16},{16,18},{18... | collective-permute-start | bytes 5192 | tf_op jit(solution)/shard_map/ppermute | solution.py:31
  282.4 4.4 %collective-permute-done.25 = f32[3,8,18,1]{3,2,1,0:T(8,128)S(1)} collective-permute-done((f32[3,8,18,1]{3,2,1,0:T(8,128)S(1)}, f32[3,8,18,1]{3,2,1,0:T(8,128)S(1)}, u32[]{:S(2)}, u32[]{:S(2)}) %collective-permute-start.25) | collective-permute-done | bytes 1760 | tf_op jit(solution)/shard_map/ppermute | solution.py:32
  290.8 5.0 %collective-permute-done.27 = f32[3,1,18,258]{3,2,1,0:T(8,128)S(1)} collective-permute-done((f32[3,1,18,258]{3,2,1,0:T(8,128)S(1)}, f32[3,1,18,258]{3,2,1,0:T(8,128)S(1)}, u32[]{:S(2)}, u32[]{:S(2)}) %collective-permute-start.27) | collective-permute-done | bytes 55760 | tf_op jit(solution)/shard_map/ppermute | solution.py:32
  303.1 7.6 %all-reduce.7 = (f32[]{:T(128)}, f32[]{:T(128)}) all-reduce(f32[]{:T(128)} %get-tuple-element.13, f32[]{:T(128)} %get-tuple-element.12), channel_id=1, replica_groups=mesh['gx_0'=4,'gx_1'=2,'gy_0'=8,'gy_1'=2,'gz'=2] {'gx_0'}, use_global_device_ids=true, to_apply=%region_25.26 | all-reduce | flops 2 | bytes 16 | tf_op jit(solution)/shard_map/psum | solution.py:20
  310.7 4.4 %all-reduce.16 = (f32[]{:T(128)}, f32[]{:T(128)}) all-reduce(f32[]{:T(128)} %get-tuple-element.24, f32[]{:T(128)} %get-tuple-element.25), channel_id=1, replica_groups=mesh['gx_0'=4,'gx_1'=2,'gy_0'=8,'gy_1'=2,'gz'=2] {'gx_1'}, use_global_device_ids=true, to_apply=%region_26.27 | all-reduce | flops 2 | bytes 16 | tf_op jit(solution)/shard_map/psum | solution.py:20
  315.1 14.0 %all-reduce.4 = (f32[]{:T(128)}, f32[]{:T(128)}) all-reduce(f32[]{:T(128)} %get-tuple-element.42, f32[]{:T(128)} %get-tuple-element.43), channel_id=1, replica_groups=mesh['gx_0'=4,'gx_1'=2,'gy_0'=8,'gy_1'=2,'gz'=2] {'gy_0'}, use_global_device_ids=true, to_apply=%region_27.28 | all-reduce | flops 2 | bytes 16 | tf_op jit(solution)/shard_map/psum | solution.py:20
  329.1 9.5 %all-reduce.13 = (f32[]{:T(128)}, f32[]{:T(128)}) all-reduce(f32[]{:T(128)} %get-tuple-element.18, f32[]{:T(128)} %get-tuple-element.19), channel_id=1, replica_groups=mesh['gx_0'=4,'gx_1'=2,'gy_0'=8,'gy_1'=2,'gz'=2] {'gy_1'}, use_global_device_ids=true, to_apply=%region_28.29 | all-reduce | flops 2 | bytes 16 | tf_op jit(solution)/shard_map/psum | solution.py:20
  338.7 5.9 %all-reduce.10 = (f32[]{:T(128)}, f32[]{:T(128)}) all-reduce(f32[]{:T(128)} %get-tuple-element.36, f32[]{:T(128)} %get-tuple-element.37), channel_id=1, replica_groups=mesh['gx_0'=4,'gx_1'=2,'gy_0'=8,'gy_1'=2,'gz'=2] {'gz'}, use_global_device_ids=true, to_apply=%region_29.30 | all-reduce | flops 2 | bytes 16 | tf_op jit(solution)/shard_map/psum | solution.py:20
  (113 shorter events, 115.9 us)
Async XLA Ops:
  24.5 5.3 %collective-permute-start = (f32[4,16,2,128]{3,1,2,0:T(8,128)S(1)}, f32[4,16,2,128]{3,1,2,0:T(8,128)S(1)}, u32[]{:S(2)}, u32[]{:S(2)}) collective-permute-start(f32[4,16,2,128]{3,1,2,0:T(8,128)S(1)} %get-tuple-element.132), channel_id=1, source_target_pairs={{0,32},{32,64},{64,96},{96,128},{128,160},{160,192},{192,224},{1,3... | collective-permute-start | bytes 196616 | tf_op jit(solution)/shard_map/ppermute | solution.py:31
  28.4 5.0 %collective-permute-start.1 = (f32[4,16,2,128]{3,1,2,0:T(8,128)S(1)}, f32[4,16,2,128]{3,1,2,0:T(8,128)S(1)}, u32[]{:S(2)}, u32[]{:S(2)}) collective-permute-start(f32[4,16,2,128]{3,1,2,0:T(8,128)S(1)} %get-tuple-element.133), channel_id=1, source_target_pairs={{32,0},{64,32},{96,64},{128,96},{160,128},{192,160},{224,192},{33,... | collective-permute-start | bytes 196616 | tf_op jit(solution)/shard_map/ppermute | solution.py:32
  34.2 8.8 %collective-permute-start.2 = (f32[4,16,20,2]{2,1,3,0:T(8,128)S(1)}, f32[4,16,20,2]{2,1,3,0:T(8,128)S(1)}, u32[]{:S(2)}, u32[]{:S(2)}) collective-permute-start(f32[4,16,20,2]{2,1,3,0:T(8,128)S(1)} %copy.202), channel_id=1, source_target_pairs={{0,1},{1,2},{2,3},{3,4},{4,5},{5,6},{6,7},{7,8},{8,9},{9,10},{10,1... | collective-permute-start | bytes 30728 | tf_op jit(solution)/shard_map/ppermute | solution.py:31
  39.2 7.3 %collective-permute-start.3 = (f32[4,16,20,2]{2,1,3,0:T(8,128)S(1)}, f32[4,16,20,2]{2,1,3,0:T(8,128)S(1)}, u32[]{:S(2)}, u32[]{:S(2)}) collective-permute-start(f32[4,16,20,2]{2,1,3,0:T(8,128)S(1)} %copy.203), channel_id=1, source_target_pairs={{1,0},{2,1},{3,2},{4,3},{5,4},{6,5},{7,6},{8,7},{9,8},{10,9},{11,1... | collective-permute-start | bytes 30728 | tf_op jit(solution)/shard_map/ppermute | solution.py:32
  65.2 4.8 %collective-permute-start.4 = (f32[2,8,1,256]{3,2,1,0:T(1,128)S(1)}, f32[2,8,1,256]{3,2,1,0:T(1,128)S(1)}, u32[]{:S(2)}, u32[]{:S(2)}) collective-permute-start(f32[2,8,1,256]{3,2,1,0:T(1,128)S(1)} %get-tuple-element.146), channel_id=1, source_target_pairs={{0,32},{32,64},{64,96},{96,128},{128,160},{160,192},{192,224},{1,3... | collective-permute-start | bytes 49160 | tf_op jit(solution)/shard_map/ppermute | solution.py:31
  68.7 4.5 %collective-permute-start.5 = (f32[2,8,1,256]{3,2,1,0:T(1,128)S(1)}, f32[2,8,1,256]{3,2,1,0:T(1,128)S(1)}, u32[]{:S(2)}, u32[]{:S(2)}) collective-permute-start(f32[2,8,1,256]{3,2,1,0:T(1,128)S(1)} %get-tuple-element.147), channel_id=1, source_target_pairs={{32,0},{64,32},{96,64},{128,96},{160,128},{192,160},{224,192},{33,... | collective-permute-start | bytes 49160 | tf_op jit(solution)/shard_map/ppermute | solution.py:32
  73.4 7.8 %collective-permute-start.6 = (f32[2,8,18,1]{3,2,1,0:T(8,128)S(1)}, f32[2,8,18,1]{3,2,1,0:T(8,128)S(1)}, u32[]{:S(2)}, u32[]{:S(2)}) collective-permute-start(f32[2,8,18,1]{3,2,1,0:T(8,128)S(1)} %get-tuple-element.142), channel_id=1, source_target_pairs={{0,2},{2,4},{4,6},{6,8},{8,10},{10,12},{12,14},{14,16},{16,18},{18... | collective-permute-start | bytes 3464 | tf_op jit(solution)/shard_map/ppermute | solution.py:31
  78.6 7.0 %collective-permute-start.7 = (f32[2,8,18,1]{3,2,1,0:T(8,128)S(1)}, f32[2,8,18,1]{3,2,1,0:T(8,128)S(1)}, u32[]{:S(2)}, u32[]{:S(2)}) collective-permute-start(f32[2,8,18,1]{3,2,1,0:T(8,128)S(1)} %get-tuple-element.143), channel_id=1, source_target_pairs={{2,0},{4,2},{6,4},{8,6},{10,8},{12,10},{14,12},{16,14},{18,16},{20... | collective-permute-start | bytes 3464 | tf_op jit(solution)/shard_map/ppermute | solution.py:32
  85.7 3.8 %collective-permute-start.8 = (f32[2,1,18,258]{3,2,1,0:T(8,128)S(1)}, f32[2,1,18,258]{3,2,1,0:T(8,128)S(1)}, u32[]{:S(2)}, u32[]{:S(2)}) collective-permute-start(f32[2,1,18,258]{3,2,1,0:T(8,128)S(1)} %get-tuple-element.122), channel_id=1, source_target_pairs={{0,1},{2,3},{4,5},{6,7},{8,9},{10,11},{12,13},{14,15},{16,17},{18,... | collective-permute-start | bytes 111464 | tf_op jit(solution)/shard_map/ppermute | solution.py:31
  87.7 6.6 %collective-permute-start.9 = (f32[2,1,18,258]{3,2,1,0:T(8,128)S(1)}, f32[2,1,18,258]{3,2,1,0:T(8,128)S(1)}, u32[]{:S(2)}, u32[]{:S(2)}) collective-permute-start(f32[2,1,18,258]{3,2,1,0:T(8,128)S(1)} %get-tuple-element.123), channel_id=1, source_target_pairs={{1,0},{3,2},{5,4},{7,6},{9,8},{11,10},{13,12},{15,14},{17,16},{19,... | collective-permute-start | bytes 111464 | tf_op jit(solution)/shard_map/ppermute | solution.py:32
  97.4 4.4 %collective-permute-start.10 = (f32[3,8,1,256]{3,2,1,0:T(1,128)S(1)}, f32[3,8,1,256]{3,2,1,0:T(1,128)S(1)}, u32[]{:S(2)}, u32[]{:S(2)}) collective-permute-start(f32[3,8,1,256]{3,2,1,0:T(1,128)S(1)} %get-tuple-element.140), channel_id=1, source_target_pairs={{0,32},{32,64},{64,96},{96,128},{128,160},{160,192},{192,224},{1,3... | collective-permute-start | bytes 73736 | tf_op jit(solution)/shard_map/ppermute | solution.py:31
  100.5 4.6 %collective-permute-start.11 = (f32[3,8,1,256]{3,2,1,0:T(1,128)S(1)}, f32[3,8,1,256]{3,2,1,0:T(1,128)S(1)}, u32[]{:S(2)}, u32[]{:S(2)}) collective-permute-start(f32[3,8,1,256]{3,2,1,0:T(1,128)S(1)} %get-tuple-element.141), channel_id=1, source_target_pairs={{32,0},{64,32},{96,64},{128,96},{160,128},{192,160},{224,192},{33,... | collective-permute-start | bytes 73736 | tf_op jit(solution)/shard_map/ppermute | solution.py:32
  105.3 8.0 %collective-permute-start.12 = (f32[3,8,18,1]{3,2,1,0:T(8,128)S(1)}, f32[3,8,18,1]{3,2,1,0:T(8,128)S(1)}, u32[]{:S(2)}, u32[]{:S(2)}) collective-permute-start(f32[3,8,18,1]{3,2,1,0:T(8,128)S(1)} %get-tuple-element.130), channel_id=1, source_target_pairs={{0,2},{2,4},{4,6},{6,8},{8,10},{10,12},{12,14},{14,16},{16,18},{18... | collective-permute-start | bytes 5192 | tf_op jit(solution)/shard_map/ppermute | solution.py:31
  109.7 8.0 %collective-permute-start.13 = (f32[3,8,18,1]{3,2,1,0:T(8,128)S(1)}, f32[3,8,18,1]{3,2,1,0:T(8,128)S(1)}, u32[]{:S(2)}, u32[]{:S(2)}) collective-permute-start(f32[3,8,18,1]{3,2,1,0:T(8,128)S(1)} %get-tuple-element.131), channel_id=1, source_target_pairs={{2,0},{4,2},{6,4},{8,6},{10,8},{12,10},{14,12},{16,14},{18,16},{20... | collective-permute-start | bytes 5192 | tf_op jit(solution)/shard_map/ppermute | solution.py:32
  117.9 3.7 %collective-permute-start.14 = (f32[3,1,18,258]{3,2,1,0:T(8,128)S(1)}, f32[3,1,18,258]{3,2,1,0:T(8,128)S(1)}, u32[]{:S(2)}, u32[]{:S(2)}) collective-permute-start(f32[3,1,18,258]{3,2,1,0:T(8,128)S(1)} %get-tuple-element.118), channel_id=1, source_target_pairs={{0,1},{2,3},{4,5},{6,7},{8,9},{10,11},{12,13},{14,15},{16,17},{18,... | collective-permute-start | bytes 167192 | tf_op jit(solution)/shard_map/ppermute | solution.py:31
  119.9 7.0 %collective-permute-start.15 = (f32[3,1,18,258]{3,2,1,0:T(8,128)S(1)}, f32[3,1,18,258]{3,2,1,0:T(8,128)S(1)}, u32[]{:S(2)}, u32[]{:S(2)}) collective-permute-start(f32[3,1,18,258]{3,2,1,0:T(8,128)S(1)} %get-tuple-element.119), channel_id=1, source_target_pairs={{1,0},{3,2},{5,4},{7,6},{9,8},{11,10},{13,12},{15,14},{17,16},{19,... | collective-permute-start | bytes 167192 | tf_op jit(solution)/shard_map/ppermute | solution.py:32
  181.9 5.0 %collective-permute-start.16 = (f32[3,8,1,256]{3,2,1,0:T(1,128)S(1)}, f32[3,8,1,256]{3,2,1,0:T(1,128)S(1)}, u32[]{:S(2)}, u32[]{:S(2)}) collective-permute-start(f32[3,8,1,256]{3,2,1,0:T(1,128)S(1)} %get-tuple-element.138), channel_id=1, source_target_pairs={{0,32},{32,64},{64,96},{96,128},{128,160},{160,192},{192,224},{1,3... | collective-permute-start | bytes 73736 | tf_op jit(solution)/shard_map/ppermute | solution.py:31
  185.6 4.6 %collective-permute-start.17 = (f32[3,8,1,256]{3,2,1,0:T(1,128)S(1)}, f32[3,8,1,256]{3,2,1,0:T(1,128)S(1)}, u32[]{:S(2)}, u32[]{:S(2)}) collective-permute-start(f32[3,8,1,256]{3,2,1,0:T(1,128)S(1)} %get-tuple-element.139), channel_id=1, source_target_pairs={{32,0},{64,32},{96,64},{128,96},{160,128},{192,160},{224,192},{33,... | collective-permute-start | bytes 73736 | tf_op jit(solution)/shard_map/ppermute | solution.py:32
  190.4 8.8 %collective-permute-start.18 = (f32[3,8,18,1]{3,2,1,0:T(8,128)S(1)}, f32[3,8,18,1]{3,2,1,0:T(8,128)S(1)}, u32[]{:S(2)}, u32[]{:S(2)}) collective-permute-start(f32[3,8,18,1]{3,2,1,0:T(8,128)S(1)} %get-tuple-element.128), channel_id=1, source_target_pairs={{0,2},{2,4},{4,6},{6,8},{8,10},{10,12},{12,14},{14,16},{16,18},{18... | collective-permute-start | bytes 5192 | tf_op jit(solution)/shard_map/ppermute | solution.py:31
  195.5 8.0 %collective-permute-start.19 = (f32[3,8,18,1]{3,2,1,0:T(8,128)S(1)}, f32[3,8,18,1]{3,2,1,0:T(8,128)S(1)}, u32[]{:S(2)}, u32[]{:S(2)}) collective-permute-start(f32[3,8,18,1]{3,2,1,0:T(8,128)S(1)} %get-tuple-element.129), channel_id=1, source_target_pairs={{2,0},{4,2},{6,4},{8,6},{10,8},{12,10},{14,12},{16,14},{18,16},{20... | collective-permute-start | bytes 5192 | tf_op jit(solution)/shard_map/ppermute | solution.py:32
  203.8 4.0 %collective-permute-start.20 = (f32[3,1,18,258]{3,2,1,0:T(8,128)S(1)}, f32[3,1,18,258]{3,2,1,0:T(8,128)S(1)}, u32[]{:S(2)}, u32[]{:S(2)}) collective-permute-start(f32[3,1,18,258]{3,2,1,0:T(8,128)S(1)} %get-tuple-element.116), channel_id=1, source_target_pairs={{0,1},{2,3},{4,5},{6,7},{8,9},{10,11},{12,13},{14,15},{16,17},{18,... | collective-permute-start | bytes 167192 | tf_op jit(solution)/shard_map/ppermute | solution.py:31
  206.0 7.0 %collective-permute-start.21 = (f32[3,1,18,258]{3,2,1,0:T(8,128)S(1)}, f32[3,1,18,258]{3,2,1,0:T(8,128)S(1)}, u32[]{:S(2)}, u32[]{:S(2)}) collective-permute-start(f32[3,1,18,258]{3,2,1,0:T(8,128)S(1)} %get-tuple-element.117), channel_id=1, source_target_pairs={{1,0},{3,2},{5,4},{7,6},{9,8},{11,10},{13,12},{15,14},{17,16},{19,... | collective-permute-start | bytes 167192 | tf_op jit(solution)/shard_map/ppermute | solution.py:32
  266.1 3.2 collective-permute-start.22
  268.1 5.5 %collective-permute-start.23 = (f32[3,8,1,256]{3,2,1,0:T(1,128)S(1)}, f32[3,8,1,256]{3,2,1,0:T(1,128)S(1)}, u32[]{:S(2)}, u32[]{:S(2)}) collective-permute-start(f32[3,8,1,256]{3,2,1,0:T(1,128)S(1)} %get-tuple-element.137), channel_id=1, source_target_pairs={{32,0},{64,32},{96,64},{128,96},{160,128},{192,160},{224,192},{33,... | collective-permute-start | bytes 73736 | tf_op jit(solution)/shard_map/ppermute | solution.py:32
  273.8 8.6 %collective-permute-start.24 = (f32[3,8,18,1]{3,2,1,0:T(8,128)S(1)}, f32[3,8,18,1]{3,2,1,0:T(8,128)S(1)}, u32[]{:S(2)}, u32[]{:S(2)}) collective-permute-start(f32[3,8,18,1]{3,2,1,0:T(8,128)S(1)} %get-tuple-element.126), channel_id=1, source_target_pairs={{0,2},{2,4},{4,6},{6,8},{8,10},{10,12},{12,14},{14,16},{16,18},{18... | collective-permute-start | bytes 5192 | tf_op jit(solution)/shard_map/ppermute | solution.py:31
  278.8 8.0 %collective-permute-start.25 = (f32[3,8,18,1]{3,2,1,0:T(8,128)S(1)}, f32[3,8,18,1]{3,2,1,0:T(8,128)S(1)}, u32[]{:S(2)}, u32[]{:S(2)}) collective-permute-start(f32[3,8,18,1]{3,2,1,0:T(8,128)S(1)} %get-tuple-element.127), channel_id=1, source_target_pairs={{2,0},{4,2},{6,4},{8,6},{10,8},{12,10},{14,12},{16,14},{18,16},{20... | collective-permute-start | bytes 5192 | tf_op jit(solution)/shard_map/ppermute | solution.py:32
  287.0 3.8 %collective-permute-start.26 = (f32[3,1,18,258]{3,2,1,0:T(8,128)S(1)}, f32[3,1,18,258]{3,2,1,0:T(8,128)S(1)}, u32[]{:S(2)}, u32[]{:S(2)}) collective-permute-start(f32[3,1,18,258]{3,2,1,0:T(8,128)S(1)} %get-tuple-element.114), channel_id=1, source_target_pairs={{0,1},{2,3},{4,5},{6,7},{8,9},{10,11},{12,13},{14,15},{16,17},{18,... | collective-permute-start | bytes 167192 | tf_op jit(solution)/shard_map/ppermute | solution.py:31
  288.8 7.0 %collective-permute-start.27 = (f32[3,1,18,258]{3,2,1,0:T(8,128)S(1)}, f32[3,1,18,258]{3,2,1,0:T(8,128)S(1)}, u32[]{:S(2)}, u32[]{:S(2)}) collective-permute-start(f32[3,1,18,258]{3,2,1,0:T(8,128)S(1)} %get-tuple-element.115), channel_id=1, source_target_pairs={{1,0},{3,2},{5,4},{7,6},{9,8},{11,10},{13,12},{15,14},{17,16},{19,... | collective-permute-start | bytes 167192 | tf_op jit(solution)/shard_map/ppermute | solution.py:32
where the time goes:
time: 351 us; the launch traced here: 350 us
  blocking collectives  140 us (40%)
  starting transfers between devices  71.6 us (20%)
  waiting for transfers between devices  65 us (19%)
  other arithmetic  52.8 us (15%)
  between operations  11.2 us (3%)
  local copies, waits for them, and re-layouts  9.35 us (3%)
    psum x15, blocking collectives, over_axes(): value = lax.psum(value, axis)  127 us
    ppermute x14, waiting for transfers between devices, padded(): after = lax.ppermute(initial, axis, down)  58.5 us
    ppermute x14, starting transfers between devices, padded(): before = lax.ppermute(last, axis, up)  48.3 us
    ppermute x14, starting transfers between devices, padded(): after = lax.ppermute(initial, axis, down)  23.3 us
    another operation x9, other arithmetic, apply_operator(): return jnp.stack(parts)  19.1 us
    another operation x2, other arithmetic, per_device(): jnp.stack([starting_kelvin, diffusive_coefficient, power, inverse_cap])  16.4 us
    all_to_all x1, blocking collectives, per_device(): lax.all_to_all(fields, 'gz', split_axis=1, concat_axis=3, tiled=True)  12.7 us
  transfers between devices with their start and end apart: 28, of which 20 were waited for; matrix products, arithmetic and copies ran while one was open for 1% of the time, Pallas kernels for 0%

commit v1 on v0

--- a/solution.py
+++ b/solution.py
@@ -17,7 +17,7 @@
 
 def over_axes(value, axes):
     for axis in axes:
-        value = lax.psum(value, axis)
+        value = jnp.sum(lax.all_gather(value, axis), axis=0)
     return value
 
 

time: 351 us -> 404 us (1.15)
  local copies, waits for them, and re-layouts: 9.35 us -> 53.7 us
  waiting for transfers between devices: 65 us -> 28 us
  starting transfers between devices: 71.6 us -> 95.3 us
  other arithmetic: 52.8 us -> 71.4 us
    unnamed x0 -> x15, blocking collectives: none -> 135 us
    psum x15 -> x0, blocking collectives: 127 us -> none  [over_axes(): value = lax.psum(value, axis)]
    ppermute x14, waiting for transfers between devices: 58.5 us -> 8.83 us  [padded(): after = lax.ppermute(initial, axis, down)]
    unnamed x1 -> x76, local copies, waits for them, and re-layouts: 0.7 us -> 45 us
    reduce_sum x0 -> x30, other arithmetic: none -> 18.5 us  [over_axes(): value = jnp.sum(lax.all_gather(value, axis), axis=0)]
    ppermute x14, waiting for transfers between devices: 6.53 us -> 19.2 us  [padded(): before = lax.ppermute(last, axis, up)]
    ppermute x14, starting transfers between devices: 23.3 us -> 35.3 us  [padded(): after = lax.ppermute(initial, axis, down)]
    ppermute x14, starting transfers between devices: 48.3 us -> 60 us  [padded(): before = lax.ppermute(last, axis, up)]
  transfers between devices with their start and end apart: 28 -> 28, of which waited for: 20 -> 18; matrix products, arithmetic and copies ran while one was open for 1% -> 1% of each run, Pallas kernels for 0% -> 0%
where the time goes in v1:
time: 404 us; the launch traced here: 402 us
  blocking collectives  143 us (35%)
  starting transfers between devices  95.3 us (24%)
  other arithmetic  71.4 us (18%)
  local copies, waits for them, and re-layouts  53.7 us (13%)
  waiting for transfers between devices  28 us (7%)
  between operations  11.1 us (3%)
    unnamed x15, blocking collectives  135 us
    ppermute x14, starting transfers between devices, padded(): before = lax.ppermute(last, axis, up)  60 us
    unnamed x76, local copies, waits for them, and re-layouts  45 us
    ppermute x14, starting transfers between devices, padded(): after = lax.ppermute(initial, axis, down)  35.3 us
    ppermute x14, waiting for transfers between devices, padded(): before = lax.ppermute(last, axis, up)  19.2 us
    another operation x9, other arithmetic, apply_operator(): return jnp.stack(parts)  19.1 us
    reduce_sum x30, other arithmetic, over_axes(): value = jnp.sum(lax.all_gather(value, axis), axis=0)  18.5 us
    another operation x2, other arithmetic, per_device(): jnp.stack([starting_kelvin, diffusive_coefficient, power, inverse_cap])  16.3 us
  transfers between devices with their start and end apart: 28, of which 18 were waited for; matrix products, arithmetic and copies ran while one was open for 1% of the time, Pallas kernels for 0%

profile of v1, /device:TPU:1, one launch (start us, length us, event | category | flops | bytes accessed | tf_op | source)
XLA Modules:
  0.0 402.0 jit_solution(13412739810825296999)
XLA Ops:
  8.1 5.1 %add_bitcast_fusion.11 = (f32[1,16,16,128]{3,1,2,0:T(8,128)S(1)}, f32[1,16,16,128]{3,1,2,0:T(8,128)S(1)}) fusion(pred[16,16,128]{2,0,1:T(8,128)(4,1)S(1)} %get-tuple-element.98, pred[16,16,128]{2,0,1:T(8,128)(4,1)S(1)} %get-tuple-element.97, pred[16,16,128]{2,0,1:T(8,128)(4,1)S(1)} %get-tuple-element.96, pred[16,16,128]{2,0,1:T(8,128)(4,1)S(1)} %get-tuple-element.95, ...), kind=kLoop, calls=%fused_computation.621 | loop fusion | flops 491520 | bytes 393248 | tf_op jit(solution)/shard_map/stack | solution.py:141
  13.2 11.2 %copy_bitcast_fusion = (f32[1,16,16,128]{3,1,2,0:T(8,128)S(1)}, f32[1,16,16,128]{3,1,2,0:T(8,128)S(1)}) fusion(f32[16,16,128]{2,1,0:T(8,128)} %param.5, f32[]{:T(128)} %bitcast.21, f32[]{:T(128)} %bitcast.20, f32[]{:T(128)} %bitcast.19, f32[]{:T(128)} %bitcast.18, f32[]{:T(128)} %bitcast.17, f32[]{:T(128)} %bitcast.16, f32[]{:T(128)} %bitcast.15, ...), kind=kLoop, calls=%fused_computation.521 | loop fusion | flops 1540096 | bytes 524352 | tf_op jit(solution)/shard_map/stack | solution.py:141
  25.7 4.6 %collective-permute-start = (f32[4,16,2,128]{3,1,2,0:T(8,128)S(1)}, f32[4,16,2,128]{3,1,2,0:T(8,128)S(1)}, u32[]{:S(2)}, u32[]{:S(2)}) collective-permute-start(f32[4,16,2,128]{3,1,2,0:T(8,128)S(1)} %get-tuple-element.132), channel_id=1, source_target_pairs={{0,32},{32,64},{64,96},{96,128},{128,160},{160,192},{192,224},{1,3... | collective-permute-start | bytes 196616 | tf_op jit(solution)/shard_map/ppermute | solution.py:31
  32.4 6.6 %collective-permute-start.3 = (f32[4,16,20,2]{2,1,3,0:T(8,128)S(1)}, f32[4,16,20,2]{2,1,3,0:T(8,128)S(1)}, u32[]{:S(2)}, u32[]{:S(2)}) collective-permute-start(f32[4,16,20,2]{2,1,3,0:T(8,128)S(1)} %copy.203), channel_id=1, source_target_pairs={{1,0},{2,1},{3,2},{4,3},{5,4},{6,5},{7,6},{8,7},{9,8},{10,9},{11,1... | collective-permute-start | bytes 30728 | tf_op jit(solution)/shard_map/ppermute | solution.py:32
  41.9 4.6 %collective-permute-done.2 = f32[4,16,20,2]{2,1,3,0:T(8,128)S(1)} collective-permute-done((f32[4,16,20,2]{2,1,3,0:T(8,128)S(1)}, f32[4,16,20,2]{2,1,3,0:T(8,128)S(1)}, u32[]{:S(2)}, u32[]{:S(2)}) %collective-permute-start.2) | collective-permute-done | bytes 10272 | tf_op jit(solution)/shard_map/ppermute | solution.py:31
  52.2 7.9 %all_to_all.18 = f32[2,16,16,128]{3,2,0,1:T(8,128)S(1)} all-to-all(f32[2,16,16,128]{3,2,0,1:T(8,128)S(1)} %copy.206), channel_id=1, replica_groups=mesh['gx_0'=4,'gx_1'=2,'gy_0'=8,'gy_1'=2,'gz'=2] {'gz'}, dimensions={1} | all-to-all | bytes 524288 | tf_op jit(solution)/shard_map/all_to_all | solution.py:156
  61.8 4.0 collective-permute-start.4
  66.9 6.4 %collective-permute-start.7 = (f32[2,8,18,1]{3,2,1,0:T(8,128)S(1)}, f32[2,8,18,1]{3,2,1,0:T(8,128)S(1)}, u32[]{:S(2)}, u32[]{:S(2)}) collective-permute-start(f32[2,8,18,1]{3,2,1,0:T(8,128)S(1)} %get-tuple-element.143), channel_id=1, source_target_pairs={{2,0},{4,2},{6,4},{8,6},{10,8},{12,10},{14,12},{16,14},{18,16},{20... | collective-permute-start | bytes 3464 | tf_op jit(solution)/shard_map/ppermute | solution.py:32
  79.5 5.5 %collective-permute-start.8 = (f32[2,1,18,258]{3,2,1,0:T(8,128)S(1)}, f32[2,1,18,258]{3,2,1,0:T(8,128)S(1)}, u32[]{:S(2)}, u32[]{:S(2)}) collective-permute-start(f32[2,1,18,258]{3,2,1,0:T(8,128)S(1)} %get-tuple-element.122), channel_id=1, source_target_pairs={{0,1},{2,3},{4,5},{6,7},{8,9},{10,11},{12,13},{14,15},{16,17},{18,... | collective-permute-start | bytes 111464 | tf_op jit(solution)/shard_map/ppermute | solution.py:31
  90.9 5.5 %collective-permute-start.10 = (f32[3,8,1,256]{3,2,1,0:T(1,128)S(1)}, f32[3,8,1,256]{3,2,1,0:T(1,128)S(1)}, u32[]{:S(2)}, u32[]{:S(2)}) collective-permute-start(f32[3,8,1,256]{3,2,1,0:T(1,128)S(1)} %get-tuple-element.140), channel_id=1, source_target_pairs={{0,32},{32,64},{64,96},{96,128},{128,160},{160,192},{192,224},{1,3... | collective-permute-start | bytes 73736 | tf_op jit(solution)/shard_map/ppermute | solution.py:31
  99.7 6.1 %collective-permute-start.12 = (f32[3,8,18,1]{3,2,1,0:T(8,128)S(1)}, f32[3,8,18,1]{3,2,1,0:T(8,128)S(1)}, u32[]{:S(2)}, u32[]{:S(2)}) collective-permute-start(f32[3,8,18,1]{3,2,1,0:T(8,128)S(1)} %get-tuple-element.130), channel_id=1, source_target_pairs={{0,2},{2,4},{4,6},{6,8},{8,10},{10,12},{12,14},{14,16},{16,18},{18... | collective-permute-start | bytes 5192 | tf_op jit(solution)/shard_map/ppermute | solution.py:31
  111.0 6.3 %collective-permute-start.14 = (f32[3,1,18,258]{3,2,1,0:T(8,128)S(1)}, f32[3,1,18,258]{3,2,1,0:T(8,128)S(1)}, u32[]{:S(2)}, u32[]{:S(2)}) collective-permute-start(f32[3,1,18,258]{3,2,1,0:T(8,128)S(1)} %get-tuple-element.118), channel_id=1, source_target_pairs={{0,1},{2,3},{4,5},{6,7},{8,9},{10,11},{12,13},{14,15},{16,17},{18,... | collective-permute-start | bytes 167192 | tf_op jit(solution)/shard_map/ppermute | solution.py:31
  131.3 13.3 %all-reduce.39 = (f32[4]{0:T(128)S(1)}, f32[4]{0:T(128)S(1)}) all-reduce(f32[4]{0:T(128)S(1)} %dynamic-update-slice, f32[4]{0:T(128)S(1)} %dynamic-update-slice.5), channel_id=1, replica_groups=mesh['gx_0'=4,'gx_1'=2,'gy_0'=8,'gy_1'=2,'gz'=2] {'gx_0'}, use_global_device_ids=true, to_apply=%add.4 | all-reduce | flops 8 | bytes 64
  157.8 16.1 %all-reduce.36 = (f32[8]{0:T(128)S(1)}, f32[8]{0:T(128)S(1)}) all-reduce(f32[8]{0:T(128)S(1)} %dynamic-update-slice.2, f32[8]{0:T(128)S(1)} %dynamic-update-slice.7), channel_id=1, replica_groups=mesh['gx_0'=4,'gx_1'=2,'gy_0'=8,'gy_1'=2,'gz'=2] {'gy_0'}, use_global_device_ids=true, to_apply=%add.6 | all-reduce | flops 16 | bytes 128
  178.4 11.0 %all-reduce.45 = (f32[2]{0:T(128)S(1)}, f32[2]{0:T(128)S(1)}) all-reduce(f32[2]{0:T(128)S(1)} %dynamic-update-slice.3, f32[2]{0:T(128)S(1)} %dynamic-update-slice.8), channel_id=1, replica_groups=mesh['gx_0'=4,'gx_1'=2,'gy_0'=8,'gy_1'=2,'gz'=2] {'gy_1'}, use_global_device_ids=true, to_apply=%add.7 | all-reduce | flops 4 | bytes 32
  193.4 5.9 %all-reduce.42 = (f32[2]{0:T(128)S(1)}, f32[2]{0:T(128)S(1)}) all-reduce(f32[2]{0:T(128)S(1)} %dynamic-update-slice.4, f32[2]{0:T(128)S(1)} %dynamic-update-slice.9), channel_id=1, replica_groups=mesh['gx_0'=4,'gx_1'=2,'gy_0'=8,'gy_1'=2,'gz'=2] {'gz'}, use_global_device_ids=true, to_apply=%add.8 | all-reduce | flops 4 | bytes 32
  203.3 4.0 collective-permute-start.16
  208.5 4.3 %collective-permute-start.19 = (f32[3,8,18,1]{3,2,1,0:T(8,128)S(1)}, f32[3,8,18,1]{3,2,1,0:T(8,128)S(1)}, u32[]{:S(2)}, u32[]{:S(2)}) collective-permute-start(f32[3,8,18,1]{3,2,1,0:T(8,128)S(1)} %get-tuple-element.129), channel_id=1, source_target_pairs={{2,0},{4,2},{6,4},{8,6},{10,8},{12,10},{14,12},{16,14},{18,16},{20... | collective-permute-start | bytes 5192 | tf_op jit(solution)/shard_map/ppermute | solution.py:32
  220.5 5.7 %collective-permute-start.20 = (f32[3,1,18,258]{3,2,1,0:T(8,128)S(1)}, f32[3,1,18,258]{3,2,1,0:T(8,128)S(1)}, u32[]{:S(2)}, u32[]{:S(2)}) collective-permute-start(f32[3,1,18,258]{3,2,1,0:T(8,128)S(1)} %get-tuple-element.116), channel_id=1, source_target_pairs={{0,1},{2,3},{4,5},{6,7},{8,9},{10,11},{12,13},{14,15},{16,17},{18,... | collective-permute-start | bytes 167192 | tf_op jit(solution)/shard_map/ppermute | solution.py:31
  237.7 8.4 %all-reduce.38 = (f32[4]{0:T(128)S(1)}, f32[4]{0:T(128)S(1)}) all-reduce(f32[4]{0:T(128)S(1)} %dynamic-update-slice.10, f32[4]{0:T(128)S(1)} %dynamic-update-slice.15), channel_id=1, replica_groups=mesh['gx_0'=4,'gx_1'=2,'gy_0'=8,'gy_1'=2,'gz'=2] {'gx_0'}, use_global_device_ids=true, to_apply=%add.14 | all-reduce | flops 8 | bytes 64
  250.1 3.8 all-reduce.47
  257.9 12.2 %all-reduce.35 = (f32[8]{0:T(128)S(1)}, f32[8]{0:T(128)S(1)}) all-reduce(f32[8]{0:T(128)S(1)} %dynamic-update-slice.12, f32[8]{0:T(128)S(1)} %dynamic-update-slice.17), channel_id=1, replica_groups=mesh['gx_0'=4,'gx_1'=2,'gy_0'=8,'gy_1'=2,'gz'=2] {'gy_0'}, use_global_device_ids=true, to_apply=%add.16 | all-reduce | flops 16 | bytes 128
  273.9 12.1 %all-reduce.44 = (f32[2]{0:T(128)S(1)}, f32[2]{0:T(128)S(1)}) all-reduce(f32[2]{0:T(128)S(1)} %dynamic-update-slice.13, f32[2]{0:T(128)S(1)} %dynamic-update-slice.18), channel_id=1, replica_groups=mesh['gx_0'=4,'gx_1'=2,'gy_0'=8,'gy_1'=2,'gz'=2] {'gy_1'}, use_global_device_ids=true, to_apply=%add.17 | all-reduce | flops 4 | bytes 32
  290.0 5.9 %all-reduce.41 = (f32[2]{0:T(128)S(1)}, f32[2]{0:T(128)S(1)}) all-reduce(f32[2]{0:T(128)S(1)} %dynamic-update-slice.14, f32[2]{0:T(128)S(1)} %dynamic-update-slice.19), channel_id=1, replica_groups=mesh['gx_0'=4,'gx_1'=2,'gy_0'=8,'gy_1'=2,'gz'=2] {'gz'}, use_global_device_ids=true, to_apply=%add.18 | all-reduce | flops 4 | bytes 32
  303.2 4.0 collective-permute-start.22
  308.3 4.3 %collective-permute-start.25 = (f32[3,8,18,1]{3,2,1,0:T(8,128)S(1)}, f32[3,8,18,1]{3,2,1,0:T(8,128)S(1)}, u32[]{:S(2)}, u32[]{:S(2)}) collective-permute-start(f32[3,8,18,1]{3,2,1,0:T(8,128)S(1)} %get-tuple-element.127), channel_id=1, source_target_pairs={{2,0},{4,2},{6,4},{8,6},{10,8},{12,10},{14,12},{16,14},{18,16},{20... | collective-permute-start | bytes 5192 | tf_op jit(solution)/shard_map/ppermute | solution.py:32
  319.6 5.8 %collective-permute-start.26 = (f32[3,1,18,258]{3,2,1,0:T(8,128)S(1)}, f32[3,1,18,258]{3,2,1,0:T(8,128)S(1)}, u32[]{:S(2)}, u32[]{:S(2)}) collective-permute-start(f32[3,1,18,258]{3,2,1,0:T(8,128)S(1)} %get-tuple-element.114), channel_id=1, source_target_pairs={{0,1},{2,3},{4,5},{6,7},{8,9},{10,11},{12,13},{14,15},{16,17},{18,... | collective-permute-start | bytes 167192 | tf_op jit(solution)/shard_map/ppermute | solution.py:31
  337.0 8.5 %all-reduce.37 = (f32[4]{0:T(128)S(1)}, f32[4]{0:T(128)S(1)}) all-reduce(f32[4]{0:T(128)S(1)} %dynamic-update-slice.20, f32[4]{0:T(128)S(1)} %dynamic-update-slice.25), channel_id=1, replica_groups=mesh['gx_0'=4,'gx_1'=2,'gy_0'=8,'gy_1'=2,'gz'=2] {'gx_0'}, use_global_device_ids=true, to_apply=%add.24 | all-reduce | flops 8 | bytes 64
  349.5 3.8 all-reduce.46
  357.4 12.0 %all-reduce.34 = (f32[8]{0:T(128)S(1)}, f32[8]{0:T(128)S(1)}) all-reduce(f32[8]{0:T(128)S(1)} %dynamic-update-slice.22, f32[8]{0:T(128)S(1)} %dynamic-update-slice.27), channel_id=1, replica_groups=mesh['gx_0'=4,'gx_1'=2,'gy_0'=8,'gy_1'=2,'gz'=2] {'gy_0'}, use_global_device_ids=true, to_apply=%add.26 | all-reduce | flops 16 | bytes 128
  373.2 12.0 %all-reduce.43 = (f32[2]{0:T(128)S(1)}, f32[2]{0:T(128)S(1)}) all-reduce(f32[2]{0:T(128)S(1)} %dynamic-update-slice.23, f32[2]{0:T(128)S(1)} %dynamic-update-slice.28), channel_id=1, replica_groups=mesh['gx_0'=4,'gx_1'=2,'gy_0'=8,'gy_1'=2,'gz'=2] {'gy_1'}, use_global_device_ids=true, to_apply=%add.27 | all-reduce | flops 4 | bytes 32
  389.9 5.9 %all-reduce.40 = (f32[2]{0:T(128)S(1)}, f32[2]{0:T(128)S(1)}) all-reduce(f32[2]{0:T(128)S(1)} %dynamic-update-slice.24, f32[2]{0:T(128)S(1)} %dynamic-update-slice.29), channel_id=1, replica_groups=mesh['gx_0'=4,'gx_1'=2,'gy_0'=8,'gy_1'=2,'gz'=2] {'gz'}, use_global_device_ids=true, to_apply=%add.28 | all-reduce | flops 4 | bytes 32
  (218 shorter events, 158.3 us)
Async XLA Ops:
  24.4 5.9 %collective-permute-start.1 = (f32[4,16,2,128]{3,1,2,0:T(8,128)S(1)}, f32[4,16,2,128]{3,1,2,0:T(8,128)S(1)}, u32[]{:S(2)}, u32[]{:S(2)}) collective-permute-start(f32[4,16,2,128]{3,1,2,0:T(8,128)S(1)} %get-tuple-element.133), channel_id=1, source_target_pairs={{32,0},{64,32},{96,64},{128,96},{160,128},{192,160},{224,192},{33,... | collective-permute-start | bytes 196616 | tf_op jit(solution)/shard_map/ppermute | solution.py:32
  25.7 5.9 %collective-permute-start = (f32[4,16,2,128]{3,1,2,0:T(8,128)S(1)}, f32[4,16,2,128]{3,1,2,0:T(8,128)S(1)}, u32[]{:S(2)}, u32[]{:S(2)}) collective-permute-start(f32[4,16,2,128]{3,1,2,0:T(8,128)S(1)} %get-tuple-element.132), channel_id=1, source_target_pairs={{0,32},{32,64},{64,96},{96,128},{128,160},{160,192},{192,224},{1,3... | collective-permute-start | bytes 196616 | tf_op jit(solution)/shard_map/ppermute | solution.py:31
  32.4 9.0 %collective-permute-start.3 = (f32[4,16,20,2]{2,1,3,0:T(8,128)S(1)}, f32[4,16,20,2]{2,1,3,0:T(8,128)S(1)}, u32[]{:S(2)}, u32[]{:S(2)}) collective-permute-start(f32[4,16,20,2]{2,1,3,0:T(8,128)S(1)} %copy.203), channel_id=1, source_target_pairs={{1,0},{2,1},{3,2},{4,3},{5,4},{6,5},{7,6},{8,7},{9,8},{10,9},{11,1... | collective-permute-start | bytes 30728 | tf_op jit(solution)/shard_map/ppermute | solution.py:32
  39.5 7.1 %collective-permute-start.2 = (f32[4,16,20,2]{2,1,3,0:T(8,128)S(1)}, f32[4,16,20,2]{2,1,3,0:T(8,128)S(1)}, u32[]{:S(2)}, u32[]{:S(2)}) collective-permute-start(f32[4,16,20,2]{2,1,3,0:T(8,128)S(1)} %copy.202), channel_id=1, source_target_pairs={{0,1},{1,2},{2,3},{3,4},{4,5},{5,6},{6,7},{7,8},{8,9},{9,10},{10,1... | collective-permute-start | bytes 30728 | tf_op jit(solution)/shard_map/ppermute | solution.py:31
  60.5 5.3 %collective-permute-start.5 = (f32[2,8,1,256]{3,2,1,0:T(1,128)S(1)}, f32[2,8,1,256]{3,2,1,0:T(1,128)S(1)}, u32[]{:S(2)}, u32[]{:S(2)}) collective-permute-start(f32[2,8,1,256]{3,2,1,0:T(1,128)S(1)} %get-tuple-element.147), channel_id=1, source_target_pairs={{32,0},{64,32},{96,64},{128,96},{160,128},{192,160},{224,192},{33,... | collective-permute-start | bytes 49160 | tf_op jit(solution)/shard_map/ppermute | solution.py:32
  61.8 4.9 %collective-permute-start.4 = (f32[2,8,1,256]{3,2,1,0:T(1,128)S(1)}, f32[2,8,1,256]{3,2,1,0:T(1,128)S(1)}, u32[]{:S(2)}, u32[]{:S(2)}) collective-permute-start(f32[2,8,1,256]{3,2,1,0:T(1,128)S(1)} %get-tuple-element.146), channel_id=1, source_target_pairs={{0,32},{32,64},{64,96},{96,128},{128,160},{160,192},{192,224},{1,3... | collective-permute-start | bytes 49160 | tf_op jit(solution)/shard_map/ppermute | solution.py:31
  66.9 10.0 %collective-permute-start.7 = (f32[2,8,18,1]{3,2,1,0:T(8,128)S(1)}, f32[2,8,18,1]{3,2,1,0:T(8,128)S(1)}, u32[]{:S(2)}, u32[]{:S(2)}) collective-permute-start(f32[2,8,18,1]{3,2,1,0:T(8,128)S(1)} %get-tuple-element.143), channel_id=1, source_target_pairs={{2,0},{4,2},{6,4},{8,6},{10,8},{12,10},{14,12},{16,14},{18,16},{20... | collective-permute-start | bytes 3464 | tf_op jit(solution)/shard_map/ppermute | solution.py:32
  73.3 4.8 %collective-permute-start.6 = (f32[2,8,18,1]{3,2,1,0:T(8,128)S(1)}, f32[2,8,18,1]{3,2,1,0:T(8,128)S(1)}, u32[]{:S(2)}, u32[]{:S(2)}) collective-permute-start(f32[2,8,18,1]{3,2,1,0:T(8,128)S(1)} %get-tuple-element.142), channel_id=1, source_target_pairs={{0,2},{2,4},{4,6},{6,8},{8,10},{10,12},{12,14},{14,16},{16,18},{18... | collective-permute-start | bytes 3464 | tf_op jit(solution)/shard_map/ppermute | solution.py:31
  78.2 7.3 %collective-permute-start.9 = (f32[2,1,18,258]{3,2,1,0:T(8,128)S(1)}, f32[2,1,18,258]{3,2,1,0:T(8,128)S(1)}, u32[]{:S(2)}, u32[]{:S(2)}) collective-permute-start(f32[2,1,18,258]{3,2,1,0:T(8,128)S(1)} %get-tuple-element.123), channel_id=1, source_target_pairs={{1,0},{3,2},{5,4},{7,6},{9,8},{11,10},{13,12},{15,14},{17,16},{19,... | collective-permute-start | bytes 111464 | tf_op jit(solution)/shard_map/ppermute | solution.py:32
  79.5 7.0 %collective-permute-start.8 = (f32[2,1,18,258]{3,2,1,0:T(8,128)S(1)}, f32[2,1,18,258]{3,2,1,0:T(8,128)S(1)}, u32[]{:S(2)}, u32[]{:S(2)}) collective-permute-start(f32[2,1,18,258]{3,2,1,0:T(8,128)S(1)} %get-tuple-element.122), channel_id=1, source_target_pairs={{0,1},{2,3},{4,5},{6,7},{8,9},{10,11},{12,13},{14,15},{16,17},{18,... | collective-permute-start | bytes 111464 | tf_op jit(solution)/shard_map/ppermute | solution.py:31
  89.6 6.8 %collective-permute-start.11 = (f32[3,8,1,256]{3,2,1,0:T(1,128)S(1)}, f32[3,8,1,256]{3,2,1,0:T(1,128)S(1)}, u32[]{:S(2)}, u32[]{:S(2)}) collective-permute-start(f32[3,8,1,256]{3,2,1,0:T(1,128)S(1)} %get-tuple-element.141), channel_id=1, source_target_pairs={{32,0},{64,32},{96,64},{128,96},{160,128},{192,160},{224,192},{33,... | collective-permute-start | bytes 73736 | tf_op jit(solution)/shard_map/ppermute | solution.py:32
  90.9 6.4 %collective-permute-start.10 = (f32[3,8,1,256]{3,2,1,0:T(1,128)S(1)}, f32[3,8,1,256]{3,2,1,0:T(1,128)S(1)}, u32[]{:S(2)}, u32[]{:S(2)}) collective-permute-start(f32[3,8,1,256]{3,2,1,0:T(1,128)S(1)} %get-tuple-element.140), channel_id=1, source_target_pairs={{0,32},{32,64},{64,96},{96,128},{128,160},{160,192},{192,224},{1,3... | collective-permute-start | bytes 73736 | tf_op jit(solution)/shard_map/ppermute | solution.py:31
  97.4 19.9 %copy-start.4 = (u32[256]{0:T(256)S(1)}, u32[256]{0:T(256)}, u32[]{:S(2)}) copy-start(u32[256]{0:T(256)} %constant.220) | copy-start | bytes 3076
  97.5 10.8 %collective-permute-start.13 = (f32[3,8,18,1]{3,2,1,0:T(8,128)S(1)}, f32[3,8,18,1]{3,2,1,0:T(8,128)S(1)}, u32[]{:S(2)}, u32[]{:S(2)}) collective-permute-start(f32[3,8,18,1]{3,2,1,0:T(8,128)S(1)} %get-tuple-element.131), channel_id=1, source_target_pairs={{2,0},{4,2},{6,4},{8,6},{10,8},{12,10},{14,12},{16,14},{18,16},{20... | collective-permute-start | bytes 5192 | tf_op jit(solution)/shard_map/ppermute | solution.py:32
  99.7 9.8 %collective-permute-start.12 = (f32[3,8,18,1]{3,2,1,0:T(8,128)S(1)}, f32[3,8,18,1]{3,2,1,0:T(8,128)S(1)}, u32[]{:S(2)}, u32[]{:S(2)}) collective-permute-start(f32[3,8,18,1]{3,2,1,0:T(8,128)S(1)} %get-tuple-element.130), channel_id=1, source_target_pairs={{0,2},{2,4},{4,6},{6,8},{8,10},{10,12},{12,14},{14,16},{16,18},{18... | collective-permute-start | bytes 5192 | tf_op jit(solution)/shard_map/ppermute | solution.py:31
  109.7 8.2 %collective-permute-start.15 = (f32[3,1,18,258]{3,2,1,0:T(8,128)S(1)}, f32[3,1,18,258]{3,2,1,0:T(8,128)S(1)}, u32[]{:S(2)}, u32[]{:S(2)}) collective-permute-start(f32[3,1,18,258]{3,2,1,0:T(8,128)S(1)} %get-tuple-element.119), channel_id=1, source_target_pairs={{1,0},{3,2},{5,4},{7,6},{9,8},{11,10},{13,12},{15,14},{17,16},{19,... | collective-permute-start | bytes 167192 | tf_op jit(solution)/shard_map/ppermute | solution.py:32
  111.0 7.9 %collective-permute-start.14 = (f32[3,1,18,258]{3,2,1,0:T(8,128)S(1)}, f32[3,1,18,258]{3,2,1,0:T(8,128)S(1)}, u32[]{:S(2)}, u32[]{:S(2)}) collective-permute-start(f32[3,1,18,258]{3,2,1,0:T(8,128)S(1)} %get-tuple-element.118), channel_id=1, source_target_pairs={{0,1},{2,3},{4,5},{6,7},{8,9},{10,11},{12,13},{14,15},{16,17},{18,... | collective-permute-start | bytes 167192 | tf_op jit(solution)/shard_map/ppermute | solution.py:31
  124.6 24.2 %copy-start.2 = (u32[256]{0:T(256)S(1)}, u32[256]{0:T(256)}, u32[]{:S(2)}) copy-start(u32[256]{0:T(256)} %constant.230) | copy-start | bytes 3076
  124.6 32.6 %copy-start.1 = (u32[256]{0:T(256)S(1)}, u32[256]{0:T(256)}, u32[]{:S(2)}) copy-start(u32[256]{0:T(256)} %constant.235) | copy-start | bytes 3076
  124.6 53.1 %copy-start = (u32[256]{0:T(256)S(1)}, u32[256]{0:T(256)}, u32[]{:S(2)}) copy-start(u32[256]{0:T(256)} %constant.240) | copy-start | bytes 3076
  202.0 5.3 %collective-permute-start.17 = (f32[3,8,1,256]{3,2,1,0:T(1,128)S(1)}, f32[3,8,1,256]{3,2,1,0:T(1,128)S(1)}, u32[]{:S(2)}, u32[]{:S(2)}) collective-permute-start(f32[3,8,1,256]{3,2,1,0:T(1,128)S(1)} %get-tuple-element.139), channel_id=1, source_target_pairs={{32,0},{64,32},{96,64},{128,96},{160,128},{192,160},{224,192},{33,... | collective-permute-start | bytes 73736 | tf_op jit(solution)/shard_map/ppermute | solution.py:32
  203.3 4.9 %collective-permute-start.16 = (f32[3,8,1,256]{3,2,1,0:T(1,128)S(1)}, f32[3,8,1,256]{3,2,1,0:T(1,128)S(1)}, u32[]{:S(2)}, u32[]{:S(2)}) collective-permute-start(f32[3,8,1,256]{3,2,1,0:T(1,128)S(1)} %get-tuple-element.138), channel_id=1, source_target_pairs={{0,32},{32,64},{64,96},{96,128},{128,160},{160,192},{192,224},{1,3... | collective-permute-start | bytes 73736 | tf_op jit(solution)/shard_map/ppermute | solution.py:31
  208.5 9.3 %collective-permute-start.19 = (f32[3,8,18,1]{3,2,1,0:T(8,128)S(1)}, f32[3,8,18,1]{3,2,1,0:T(8,128)S(1)}, u32[]{:S(2)}, u32[]{:S(2)}) collective-permute-start(f32[3,8,18,1]{3,2,1,0:T(8,128)S(1)} %get-tuple-element.129), channel_id=1, source_target_pairs={{2,0},{4,2},{6,4},{8,6},{10,8},{12,10},{14,12},{16,14},{18,16},{20... | collective-permute-start | bytes 5192 | tf_op jit(solution)/shard_map/ppermute | solution.py:32
  212.7 6.3 %collective-permute-start.18 = (f32[3,8,18,1]{3,2,1,0:T(8,128)S(1)}, f32[3,8,18,1]{3,2,1,0:T(8,128)S(1)}, u32[]{:S(2)}, u32[]{:S(2)}) collective-permute-start(f32[3,8,18,1]{3,2,1,0:T(8,128)S(1)} %get-tuple-element.128), channel_id=1, source_target_pairs={{0,2},{2,4},{4,6},{6,8},{8,10},{10,12},{12,14},{14,16},{16,18},{18... | collective-permute-start | bytes 5192 | tf_op jit(solution)/shard_map/ppermute | solution.py:31
  219.2 7.0 %collective-permute-start.21 = (f32[3,1,18,258]{3,2,1,0:T(8,128)S(1)}, f32[3,1,18,258]{3,2,1,0:T(8,128)S(1)}, u32[]{:S(2)}, u32[]{:S(2)}) collective-permute-start(f32[3,1,18,258]{3,2,1,0:T(8,128)S(1)} %get-tuple-element.117), channel_id=1, source_target_pairs={{1,0},{3,2},{5,4},{7,6},{9,8},{11,10},{13,12},{15,14},{17,16},{19,... | collective-permute-start | bytes 167192 | tf_op jit(solution)/shard_map/ppermute | solution.py:32
  220.5 7.2 %collective-permute-start.20 = (f32[3,1,18,258]{3,2,1,0:T(8,128)S(1)}, f32[3,1,18,258]{3,2,1,0:T(8,128)S(1)}, u32[]{:S(2)}, u32[]{:S(2)}) collective-permute-start(f32[3,1,18,258]{3,2,1,0:T(8,128)S(1)} %get-tuple-element.116), channel_id=1, source_target_pairs={{0,1},{2,3},{4,5},{6,7},{8,9},{10,11},{12,13},{14,15},{16,17},{18,... | collective-permute-start | bytes 167192 | tf_op jit(solution)/shard_map/ppermute | solution.py:31
  301.9 5.3 %collective-permute-start.23 = (f32[3,8,1,256]{3,2,1,0:T(1,128)S(1)}, f32[3,8,1,256]{3,2,1,0:T(1,128)S(1)}, u32[]{:S(2)}, u32[]{:S(2)}) collective-permute-start(f32[3,8,1,256]{3,2,1,0:T(1,128)S(1)} %get-tuple-element.137), channel_id=1, source_target_pairs={{32,0},{64,32},{96,64},{128,96},{160,128},{192,160},{224,192},{33,... | collective-permute-start | bytes 73736 | tf_op jit(solution)/shard_map/ppermute | solution.py:32
  303.2 4.9 %collective-permute-start.22 = (f32[3,8,1,256]{3,2,1,0:T(1,128)S(1)}, f32[3,8,1,256]{3,2,1,0:T(1,128)S(1)}, u32[]{:S(2)}, u32[]{:S(2)}) collective-permute-start(f32[3,8,1,256]{3,2,1,0:T(1,128)S(1)} %get-tuple-element.136), channel_id=1, source_target_pairs={{0,32},{32,64},{64,96},{96,128},{128,160},{160,192},{192,224},{1,3... | collective-permute-start | bytes 73736 | tf_op jit(solution)/shard_map/ppermute | solution.py:31
  308.3 8.7 %collective-permute-start.25 = (f32[3,8,18,1]{3,2,1,0:T(8,128)S(1)}, f32[3,8,18,1]{3,2,1,0:T(8,128)S(1)}, u32[]{:S(2)}, u32[]{:S(2)}) collective-permute-start(f32[3,8,18,1]{3,2,1,0:T(8,128)S(1)} %get-tuple-element.127), channel_id=1, source_target_pairs={{2,0},{4,2},{6,4},{8,6},{10,8},{12,10},{14,12},{16,14},{18,16},{20... | collective-permute-start | bytes 5192 | tf_op jit(solution)/shard_map/ppermute | solution.py:32
  312.6 5.6 %collective-permute-start.24 = (f32[3,8,18,1]{3,2,1,0:T(8,128)S(1)}, f32[3,8,18,1]{3,2,1,0:T(8,128)S(1)}, u32[]{:S(2)}, u32[]{:S(2)}) collective-permute-start(f32[3,8,18,1]{3,2,1,0:T(8,128)S(1)} %get-tuple-element.126), channel_id=1, source_target_pairs={{0,2},{2,4},{4,6},{6,8},{8,10},{10,12},{12,14},{14,16},{16,18},{18... | collective-permute-start | bytes 5192 | tf_op jit(solution)/shard_map/ppermute | solution.py:31
  318.3 7.1 %collective-permute-start.27 = (f32[3,1,18,258]{3,2,1,0:T(8,128)S(1)}, f32[3,1,18,258]{3,2,1,0:T(8,128)S(1)}, u32[]{:S(2)}, u32[]{:S(2)}) collective-permute-start(f32[3,1,18,258]{3,2,1,0:T(8,128)S(1)} %get-tuple-element.115), channel_id=1, source_target_pairs={{1,0},{3,2},{5,4},{7,6},{9,8},{11,10},{13,12},{15,14},{17,16},{19,... | collective-permute-start | bytes 167192 | tf_op jit(solution)/shard_map/ppermute | solution.py:32
  319.6 7.2 %collective-permute-start.26 = (f32[3,1,18,258]{3,2,1,0:T(8,128)S(1)}, f32[3,1,18,258]{3,2,1,0:T(8,128)S(1)}, u32[]{:S(2)}, u32[]{:S(2)}) collective-permute-start(f32[3,1,18,258]{3,2,1,0:T(8,128)S(1)} %get-tuple-element.114), channel_id=1, source_target_pairs={{0,1},{2,3},{4,5},{6,7},{8,9},{10,11},{12,13},{14,15},{16,17},{18,... | collective-permute-start | bytes 167192 | tf_op jit(solution)/shard_map/ppermute | solution.py:31
  (1 other events, 6.2 us)
